TPU v7x, 32 devices: a whole 2x2x4 slice. The times are simulated.
32 devices in a mesh: dp: 8 (over y, x, core), vocab: 4 (over z).
Axes of the slice: x: 2, y: 2, z: 4, core: 2. Of those that a mesh axis runs over, the one named last changes fastest.
Arguments:
- hidden: bfloat16 [64, 4096], P('dp'), may hold values from -16 to 16
- embed_grad: bfloat16 [64, 4096], P('dp'), may hold values from -3 to 3
- token_ids: int32 [64], P('dp'), may hold values from 0 to 32767
- loss_weight: float32 [64], P('dp'), may hold values from 16 to 256
- teacher_logits: bfloat16 [64, 32768], P('dp', 'vocab'), may hold values from -24 to 256
- head: bfloat16 [4096, 32768], P('dp', 'vocab'), may hold values from -1 to 1
Outputs:
- grad_hidden: bfloat16 [64, 4096], P('dp', 'vocab')
- head_grad: float32 [4096, 32768], P('dp', 'vocab')
Inputs may be any that keep to these rules, and one draw needn't show every extreme that they name: `token_ids`: token ids of the vocabulary window.
All inputs are finite; a program needn't handle non-finite values.
Results may differ from a plain program's by a relative error of at most 0.0022.
The roundings to bfloat16 on the way count: a program that leaves them out, or rounds other values in their place, can miss the bound.
Values may be sent and summed in bfloat16 or wider, within the bound.
A program may use at most 128 MiB of HBM per device.

v0:
```python
import jax
import jax.numpy as jnp
from jax import lax
from jax.sharding import PartitionSpec as P


def combined_all(part, axis, combine):
    gathered = jax.tree.map(lambda a: lax.all_gather(a, axis), part)

    def take(source):
        return jax.tree.map(lambda a: lax.dynamic_index_in_dim(a, source, 0, False), gathered)

    return lax.fori_loop(
        1, lax.axis_size(axis), lambda source, state: combine(state, take(source)), take(0)
    )


def contract_rows(left, right):
    return lax.dot_general(
        left, right, (((0,), (0,)), ((), ())), preferred_element_type=jnp.float32
    )


def contract_cols(left, right):
    return lax.dot_general(
        left, right, (((1,), (1,)), ((), ())), preferred_element_type=jnp.float32
    )


def combine_pairs(earlier, later):
    s_max_a, s_sum_a, t_max_a, t_sum_a = earlier
    s_max_b, s_sum_b, t_max_b, t_sum_b = later
    s_max = jnp.maximum(s_max_a, s_max_b)
    t_max = jnp.maximum(t_max_a, t_max_b)
    s_sum = s_sum_a * jnp.exp(s_max_a - s_max) + s_sum_b * jnp.exp(s_max_b - s_max)
    t_sum = t_sum_a * jnp.exp(t_max_a - t_max) + t_sum_b * jnp.exp(t_max_b - t_max)
    return (s_max, s_sum, t_max, t_sum)


def per_device(hidden, embed_grad, token_ids, loss_weight, teacher_logits, head):
    vocab_width = head.shape[1]
    hidden_cols, embed_cols = (
        lax.all_to_all(hidden, "dp", split_axis=1, concat_axis=0, tiled=True),
        lax.all_to_all(embed_grad, "dp", split_axis=1, concat_axis=0, tiled=True),
    )
    student = lax.psum_scatter(
        jnp.dot(hidden_cols, head, preferred_element_type=jnp.float32),
        "dp",
        scatter_dimension=0,
        tiled=True,
    )
    teacher = teacher_logits.astype(jnp.float32)
    student_max = jnp.max(student, axis=1)
    teacher_max = jnp.max(teacher, axis=1)
    student_sum = jnp.sum(jnp.exp(student - student_max[:, None]), axis=1)
    teacher_sum = jnp.sum(jnp.exp(teacher - teacher_max[:, None]), axis=1)
    student_top, student_total, teacher_top, teacher_total = combined_all(
        (student_max, student_sum, teacher_max, teacher_sum), "vocab", combine_pairs
    )
    student_norm = student_top + jnp.log(student_total)
    teacher_norm = teacher_top + jnp.log(teacher_total)
    gap = (
        loss_weight[:, None]
        * (jnp.exp(student - student_norm[:, None]) - jnp.exp(teacher - teacher_norm[:, None]))
    ).astype(jnp.bfloat16)
    vocab_ids = lax.axis_index("vocab") * vocab_width + jnp.arange(vocab_width, dtype=jnp.int32)
    gap_piece = lax.all_gather(gap, "dp", axis=0, tiled=True)
    id_piece = lax.all_gather(token_ids, "dp", axis=0, tiled=True)
    lookup = (id_piece[:, None] == vocab_ids[None, :]).astype(jnp.bfloat16)
    grad_rows = contract_rows(hidden_cols, gap_piece) + contract_rows(embed_cols, lookup)
    back_cols = contract_cols(gap_piece, head)
    head_grad, back_cols = (grad_rows, back_cols)
    regrouped = lax.all_to_all(back_cols, "dp", split_axis=0, concat_axis=1, tiled=True)
    grad_hidden = lax.psum_scatter(regrouped, "vocab", scatter_dimension=1, tiled=True).astype(
        jnp.bfloat16
    )
    return (grad_hidden, head_grad)


def solution(mesh):
    placed = (P("dp", None), P("dp", None), P("dp"), P("dp"), P("dp", "vocab"), P("dp", "vocab"))
    return jax.shard_map(
        per_device,
        mesh=mesh,
        in_specs=placed,
        out_specs=(P("dp", "vocab"), P("dp", "vocab")),
        check_vma=False,
    )
```

profile of v0, /device:TPU:0, one launch (start us, length us, event | category | flops | bytes accessed | tf_op | source)
XLA Modules:
  0.0 173.7 jit_solution(2264943251010884728)
XLA Ops:
  7.2 0.0 reduce-scatter.3.cloned.1.call-start
  7.2 10.2 %all_to_all.57 = bf16[8,8,512]{2,0,1:T(8,128)(2,1)S(1)} all-to-all(bf16[8,8,512]{2,0,1:T(8,128)(2,1)} %bitcast.60), channel_id=1, replica_groups=mesh['dp'=8,'vocab'=4] {'dp'}, dimensions={1} | all-to-all | bytes 131072 | tf_op jit(solution)/shard_map/all_to_all | solution.py:43
  17.4 0.0 copy-start.1
  17.4 0.0 copy-start.6
  17.4 6.3 %fusion.22 = f32[64,8192]{1,0:T(8,128)} fusion(bf16[512,8192]{1,0:T(8,128)(2,1)} %param.13, bf16[8,8,512]{2,0,1:T(8,128)(2,1)S(1)} %all_to_all.57), kind=kOutput, calls=%fused_computation.31 | convolution fusion | flops 536870912 | bytes 10551296 | tf_op jit(solution)/shard_map/dot_general | solution.py:47
  23.8 0.0 reduce-scatter.3.cloned.1.call-update
  23.8 0.0 all-gather.6.cloned.1.call-start
  23.8 0.0 copy-done.1
  23.8 0.2 reduce_max.28
  24.0 0.0 copy-done.6
  24.0 0.6 dynamic-slice
  25.3 0.3 fusion.14
  25.6 0.2 dynamic-update-slice.3
  25.8 0.1 convert_dynamic-update-slice_fusion
  25.9 38.6 %reduce-scatter.3.cloned.1.call-done = f32[8,8192]{1,0:T(8,128)} async-done(((f32[64,8192]{1,0:T(8,128)}), f32[8,8192]{1,0:T(8,128)}) %reduce-scatter.3.cloned.1.call-update) | async-done | bytes 262160 | tf_op jit(solution)/shard_map/reduce_scatter | solution.py:46
  64.5 1.1 reduce_max.27
  65.6 0.2 dynamic-update-slice
  65.8 1.2 exponential_reduce_fusion
  67.0 0.2 dynamic-update-slice.1
  67.3 11.7 %all-reduce.5 = (f32[32]{0:T(128)S(1)}, f32[32]{0:T(128)S(1)}, f32[32]{0:T(128)S(1)}, f32[32]{0:T(128)S(1)}) all-reduce(f32[32]{0:T(128)S(1)} %dynamic-update-slice, f32[32]{0:T(128)S(1)} %dynamic-update-slice.1, f32[32]{0:T(128)S(1)} %convert_dynamic-update-slice_fusion, ...), channel_id=2, replica_groups=mesh['dp'=8,'vocab'=4] {'vocab'}, use_global_device_ids=true, to_apply=%add | all-reduce | flops 128 | bytes 1024
  78.9 0.1 reshape.35
  79.0 0.1 reshape.36
  79.1 0.1 reshape.37
  79.2 0.1 reshape.38
  79.3 0.1 while.21
  79.4 0.0 copy-done.3
  79.4 1.8 %fusion.18 = bf16[8,8192]{1,0:T(8,128)(2,1)} fusion(bf16[8,8192]{1,0:T(8,128)(2,1)S(1)} %copy-done.1, f32[8,8192]{1,0:T(8,128)} %reduce-scatter.3.cloned.1.call-done, f32[8]{0:T(128)S(1)} %get-tuple-element.259, f32[8]{0:T(128)S(1)} %get-tuple-element.260, f32[8]{0:T(128)S(1)} %copy-done.3), kind=kLoop, calls=%fused_computation.26 | loop fusion | flops 393216 | bytes 524384 | tf_op jit(solution)/shard_map/convert_element_type | solution.py:65
  81.2 0.0 all-gather.6.cloned.1.call-update
  81.2 20.8 %all-gather.6.cloned.1.call-done = bf16[64,8192]{1,0:T(8,128)(2,1)} async-done(((bf16[8,8192]{1,0:T(8,128)(2,1)}), bf16[64,8192]{1,0:T(8,128)(2,1)}) %all-gather.6.cloned.1.call-update) | async-done | bytes 1048592 | tf_op jit(solution)/shard_map/all_gather | solution.py:67
  102.0 7.1 %convolution_bitcast_fusion = f32[8,8,512]{2,1,0:T(8,128)} fusion(bf16[64,8192]{1,0:T(8,128)(2,1)} %all-gather.6.cloned.1.call-done, bf16[512,8192]{1,0:T(8,128)(2,1)} %param.13), kind=kOutput, calls=%fused_computation.16 | convolution fusion | flops 536870912 | bytes 9568256 | tf_op jit(solution)/shard_map/dot_general | solution.py:25
  109.1 3.4 %all-to-all-start.1 = ((f32[8,8,512]{2,1,0:T(8,128)}), f32[8,8,512]{2,1,0:T(8,128)S(1)}, u32[]{:S(2)}, u32[]{:S(2)}) async-start(f32[8,8,512]{2,1,0:T(8,128)} %convolution_bitcast_fusion), calls=%async_computation.2 | async-start | bytes 262144 | tf_op jit(solution)/shard_map/all_to_all | solution.py:73
  112.5 0.0 copy-done.5
  112.5 0.6 dynamic-slice.4
  113.7 0.0 copy-done.4
  113.7 0.2 dynamic-update-slice.4
  114.0 8.4 %all-reduce.4 = s32[64]{0:T(128)S(1)} all-reduce(s32[64]{0:T(128)S(1)} %dynamic-update-slice.4), channel_id=1, replica_groups=mesh['dp'=8,'vocab'=4] {'dp'}, use_global_device_ids=true, to_apply=%add.4 | all-reduce | flops 64 | bytes 512
  122.4 0.0 all-to-all-done.1
  122.4 0.0 copy-start.2
  122.4 3.4 %all-to-all-start.2 = ((bf16[8,8,512]{2,0,1:T(8,128)(2,1)}), bf16[8,8,512]{2,0,1:T(8,128)(2,1)S(1)}, u32[]{:S(2)}, u32[]{:S(2)}) async-start(bf16[8,8,512]{2,0,1:T(8,128)(2,1)} %bitcast.13), calls=%async_computation.4 | async-start | bytes 131072 | tf_op jit(solution)/shard_map/all_to_all | solution.py:44
  125.8 0.0 reduce-scatter.5.cloned.1.call-start
  125.8 0.0 copy-done
  125.8 8.5 %fusion.20 = f32[8192,512]{1,0:T(8,128)} fusion(bf16[64,8192]{1,0:T(8,128)(2,1)S(1)} %copy-done, bf16[8,8,512]{2,0,1:T(8,128)(2,1)S(1)} %all_to_all.57), kind=kOutput, calls=%fused_computation.29 | convolution fusion | flops 536870912 | bytes 17891328 | tf_op jit(solution)/shard_map/dot_general | solution.py:19
  134.4 0.0 copy-done.2
  134.4 0.0 reduce-scatter.5.cloned.1.call-update
  134.4 0.0 all-to-all-done.2
  134.4 13.9 %add_bitcast_fusion = f32[512,8192]{0,1:T(8,128)} fusion(f32[8192,512]{1,0:T(8,128)} %fusion.20, s32[8192]{0:T(1024)S(1)} %iota_add_fusion, s32[64]{0:T(128)S(1)} %all-reduce.4, bf16[8,8,512]{2,0,1:T(8,128)(2,1)S(1)} %all-to-all-done.2), kind=kOutput, calls=%fused_computation.14 | convolution fusion | flops 541589504 | bytes 33652992 | tf_op jit(solution)/shard_map/dot_general | solution.py:19
  148.4 17.4 %copy.8 = f32[512,8192]{1,0:T(8,128)} copy(f32[512,8192]{0,1:T(8,128)} %add_bitcast_fusion) | data formatting | bytes 33554432
  165.8 1.4 convert_element_type.12
  (16 shorter events, 0.1 us)
Async XLA Ops:
  7.2 57.3 %reduce-scatter.3.cloned.1.call-start = ((), (), s32[]{:S(2)}) async-start(), calls=%async_computation.5 | async-start | bytes 2359296 | tf_op jit(solution)/shard_map/reduce_scatter | solution.py:46
  17.4 6.4 %copy-start.1 = (bf16[8,8192]{1,0:T(8,128)(2,1)S(1)}, bf16[8,8192]{1,0:T(8,128)(2,1)}, u32[]{:S(2)}) copy-start(bf16[8,8192]{1,0:T(8,128)(2,1)} %param.12) | copy-start | bytes 393220
  17.4 6.6 %copy-start.6 = (u32[32]{0:T(128)S(1)}, u32[32]{0:T(128)}, u32[]{:S(2)}) copy-start(u32[32]{0:T(128)} %constant.69) | copy-start | bytes 388
  17.4 62.0 %copy-start.3 = (f32[8]{0:T(128)S(1)}, f32[8]{0:T(128)}, u32[]{:S(2)}) copy-start(f32[8]{0:T(128)} %param.11) | copy-start | bytes 100
  23.7 88.7 %copy-start.5 = (u32[32]{0:T(128)S(1)}, u32[32]{0:T(128)}, u32[]{:S(2)}) copy-start(u32[32]{0:T(128)} %constant.89) | copy-start | bytes 388
  23.7 90.0 %copy-start.4 = (s32[8]{0:T(128)S(1)}, s32[8]{0:T(128)}, u32[]{:S(2)}) copy-start(s32[8]{0:T(128)} %param.10) | copy-start | bytes 100
  23.8 78.2 %all-gather.6.cloned.1.call-start = ((), (), s32[]{:S(2)}) async-start(), calls=%async_computation.6 | async-start | bytes 1179648 | tf_op jit(solution)/shard_map/all_gather | solution.py:67
  102.0 23.9 %copy-start = (bf16[64,8192]{1,0:T(8,128)(2,1)S(1)}, bf16[64,8192]{1,0:T(8,128)(2,1)}, u32[]{:S(2)}) copy-start(bf16[64,8192]{1,0:T(8,128)(2,1)} %all-gather.6.cloned.1.call-done) | copy-start | bytes 3145732
  109.1 13.3 %all-to-all-start.1 = ((f32[8,8,512]{2,1,0:T(8,128)}), f32[8,8,512]{2,1,0:T(8,128)S(1)}, u32[]{:S(2)}, u32[]{:S(2)}) async-start(f32[8,8,512]{2,1,0:T(8,128)} %convolution_bitcast_fusion), calls=%async_computation.2 | async-start | bytes 262144 | tf_op jit(solution)/shard_map/all_to_all | solution.py:73
  122.4 12.0 %copy-start.2 = (f32[8,8,512]{2,1,0:T(8,128)}, f32[8,8,512]{2,1,0:T(8,128)S(1)}, u32[]{:S(2)}) copy-start(f32[8,8,512]{2,1,0:T(8,128)S(1)} %all-to-all-done.1) | copy-start | bytes 393220
  122.4 12.0 %all-to-all-start.2 = ((bf16[8,8,512]{2,0,1:T(8,128)(2,1)}), bf16[8,8,512]{2,0,1:T(8,128)(2,1)S(1)}, u32[]{:S(2)}, u32[]{:S(2)}) async-start(bf16[8,8,512]{2,0,1:T(8,128)(2,1)} %bitcast.13), calls=%async_computation.4 | async-start | bytes 131072 | tf_op jit(solution)/shard_map/all_to_all | solution.py:44
  125.8 40.0 %reduce-scatter.5.cloned.1.call-start = ((), (), s32[]{:S(2)}) async-start(), calls=%async_computation.7 | async-start | bytes 163840 | tf_op jit(solution)/shard_map/reduce_scatter | solution.py:74
Sparse Core Ops, SparseCore 0:
  23.9 40.5 reduce-scatter.2
  81.3 20.5 all-gather.5
  134.5 20.7 reduce-scatter.4
where the time goes:
time: 175 us; the launch traced here: 174 us
  waiting for transfers between devices  59.4 us (34%)
  matrix products  35.9 us (21%)
  blocking collectives  30.3 us (17%)
  local copies, waits for them, and re-layouts  20 us (11%)
  between operations  15.2 us (9%)
  starting transfers between devices  6.86 us (4%)
  other arithmetic  6.1 us (3%)
    reduce_scatter x1, waiting for transfers between devices, per_device(): lax.psum_scatter(jnp.dot(hidden_cols, head, preferred_element_type=jnp.fl...  38.6 us
    dot_general x2, matrix products, contract_rows(): lax.dot_general(left, right, (((0,), (0,)), ((), ())), preferred_element_...  22.5 us
    all_gather x1, waiting for transfers between devices, per_device(): gap_piece = lax.all_gather(gap, 'dp', axis=0, tiled=True)  20.8 us
    unnamed x2, blocking collectives  20.1 us
    unnamed x26, local copies, waits for them, and re-layouts  19.6 us
    all_to_all x1, blocking collectives, per_device(): lax.all_to_all(hidden, 'dp', split_axis=1, concat_axis=0, tiled=True)  10.2 us
    dot_general x1, matrix products, contract_cols(): lax.dot_general(left, right, (((1,), (1,)), ((), ())), preferred_element_...  7.1 us
    dot_general x1, matrix products, per_device(): jnp.dot(hidden_cols, head, preferred_element_type=jnp.float32)  6.31 us
  transfers between devices with their start and end apart: 5, of which 2 were waited for; matrix products, arithmetic and copies ran while one was open for 24% of the time, Pallas kernels for 0%

commit v1 on v0

v1 whole, which is shorter than its diff:
```python
import functools

import jax
import jax.numpy as jnp
from jax import lax
from jax.experimental import pallas as pl
from jax.experimental.pallas import tpu as pltpu
from jax.sharding import PartitionSpec as P

MESH = pl.DeviceIdType.MESH
F32 = jnp.float32
BF16 = jnp.bfloat16


def flat_rows(block):
    return block.astype(F32).reshape(block.shape[0] * block.shape[1], block.shape[2]).astype(BF16)


def comm_kernel(
    n, nv, chunks, pieces,
    hidden, embed, ids, weight, teacher, head,
    grad_out, gap_out, hid_out, emb_out, ids_out,
    hc, ec, idt, tea, head_v, hx, part, xbuf, total, rsbuf, stu, stat, ga, bk, fin,
    head_sem, tea_sem, own_sem, out_sem,
    hid_s, hid_r, emb_s, emb_r, ids_s, ids_r,
    pair_s, pair_r, rs_s, rs_r, st_s, st_r, ag_s, ag_r, fw_s, fw_r, fin_s, fin_r,
):
    i = lax.axis_index("dp")
    v = lax.axis_index("vocab")
    nc = n // 2
    core = lax.rem(i, 2)
    chip = lax.div(i, 2)
    partner = i + 1 - 2 * core
    rows, vocab = teacher.shape
    width = vocab // chunks
    cut = vocab // pieces
    group = n // nv

    def slot(j):
        return lax.rem(j, 2) * nc + lax.div(j, 2)

    mine = slot(i)

    def remote(src, dst, send, recv, dp, vo=None):
        return pltpu.make_async_remote_copy(
            src_ref=src, dst_ref=dst, send_sem=send, recv_sem=recv,
            device_id=(dp, v if vo is None else vo), device_id_type=MESH,
        )

    barrier = pltpu.get_barrier_semaphore()
    for dd in range(n):
        for dv in range(nv):
            if dd or dv:
                pl.semaphore_signal(
                    barrier, inc=1,
                    device_id=(lax.rem(i + dd, n), lax.rem(v + dv, nv)),
                    device_id_type=MESH,
                )

    own = [
        pltpu.make_async_copy(hidden.at[i], hc.at[mine], own_sem.at[0]),
        pltpu.make_async_copy(embed.at[i], ec.at[mine], own_sem.at[1]),
    ]
    for copy in own:
        copy.start()
    heads = []
    for ch in range(chunks):
        cols = pl.ds(ch * width, width)
        heads.append(pltpu.make_async_copy(head.at[:, cols], head_v.at[:, cols], head_sem.at[ch]))
        heads[-1].start()
    tea_copy = pltpu.make_async_copy(teacher, tea, tea_sem)
    tea_copy.start()

    row = lax.broadcasted_iota(jnp.int32, (rows, 128), 0)
    id_tile = jnp.zeros((rows, 128), jnp.int32)
    w_tile = jnp.zeros((rows, 128), F32)
    for r in range(rows):
        id_tile = jnp.where(row == r, ids[r], id_tile)
        w_tile = jnp.where(row == r, weight[r], w_tile)
    idt[mine] = id_tile
    w_col = w_tile[:, 0:1]

    pl.semaphore_wait(barrier, n * nv - 1)

    hid, emb, idc = [], [], []
    for d in range(1, n):
        j = lax.rem(i + d, n)
        hid.append(remote(hidden.at[j], hc.at[mine], hid_s.at[d], hid_r.at[d], j))
        hid[-1].start()
    for d in range(1, n):
        j = lax.rem(i + d, n)
        emb.append(remote(embed.at[j], ec.at[mine], emb_s.at[d], emb_r.at[d], j))
        idc.append(remote(idt.at[mine], idt.at[mine], ids_s.at[d], ids_r.at[d], j))
        emb[-1].start()
        idc[-1].start()

    own[0].wait()
    for copy in hid:
        copy.wait_recv()
    hx[...] = flat_rows(hc[...])
    hid_copy = pltpu.make_async_copy(hc, hid_out, out_sem.at[0])
    hid_copy.start()

    pair, rs = [], []

    def reduce_pair(ch):
        pair[ch].wait_recv()
        total[ch] = part[ch, core] + xbuf[ch]
        sends = []
        for d in range(1, nc):
            k = lax.rem(chip + d, nc)
            sends.append(
                remote(total.at[ch, k], rsbuf.at[ch, d], rs_s.at[ch, d], rs_r.at[ch, d], 2 * k + core)
            )
            sends[-1].start()
        rs.append(sends)

    for ch in range(chunks):
        heads[ch].wait()
        product = jnp.dot(
            hx[...], head_v[:, ch * width:(ch + 1) * width], preferred_element_type=F32
        )
        part[ch] = product.reshape(2, nc, rows, width)
        pair.append(remote(part.at[ch, 1 - core], xbuf.at[ch], pair_s.at[ch], pair_r.at[ch], partner))
        pair[ch].start()
        if ch:
            reduce_pair(ch - 1)
    reduce_pair(chunks - 1)

    tea_copy.wait()
    t = tea[...].astype(F32)
    t_max = jnp.max(t, axis=1, keepdims=True)
    t_sum = jnp.sum(jnp.exp(t - t_max), axis=1, keepdims=True)

    own[1].wait()
    for copy in emb + idc:
        copy.wait_recv()
    emb_copy = pltpu.make_async_copy(ec, emb_out, out_sem.at[1])
    ids_copy = pltpu.make_async_copy(idt, ids_out, out_sem.at[2])
    emb_copy.start()
    ids_copy.start()

    s_max = None
    for ch in range(chunks):
        s = total[ch, chip]
        for d in range(1, nc):
            rs[ch][d - 1].wait_recv()
            s = s + rsbuf[ch, d]
        stu[:, ch * width:(ch + 1) * width] = s
        top = jnp.max(s, axis=1, keepdims=True)
        s_max = top if s_max is None else jnp.maximum(s_max, top)
    s_sum = jnp.sum(jnp.exp(stu[...] - s_max), axis=1, keepdims=True)

    lane = lax.broadcasted_iota(jnp.int32, (rows, 128), 1)
    stat[0] = jnp.where(
        lane == 0, s_max, jnp.where(lane == 1, s_sum, jnp.where(lane == 2, t_max, t_sum))
    )
    sts = []
    for d in range(1, nv):
        sts.append(
            remote(stat.at[0], stat.at[d], st_s.at[d], st_r.at[d], i, lax.rem(v + d, nv))
        )
        sts[-1].start()
    for copy in sts:
        copy.wait_recv()
    s_tops = [stat[d][:, 0:1] for d in range(nv)]
    t_tops = [stat[d][:, 2:3] for d in range(nv)]
    s_top = functools.reduce(jnp.maximum, s_tops)
    t_top = functools.reduce(jnp.maximum, t_tops)
    s_tot = sum(stat[d][:, 1:2] * jnp.exp(s_tops[d] - s_top) for d in range(nv))
    t_tot = sum(stat[d][:, 3:4] * jnp.exp(t_tops[d] - t_top) for d in range(nv))
    s_norm = s_top + jnp.log(s_tot)
    t_norm = t_top + jnp.log(t_tot)

    ag, fw = [], []
    for g in range(pieces):
        cols = pl.ds(g * cut, cut)
        gap = w_col * (
            jnp.exp(stu[:, cols] - s_norm) - jnp.exp(tea[:, cols].astype(F32) - t_norm)
        )
        ga[mine, :, cols] = gap.astype(BF16)
        block = ga.at[mine, :, cols]
        sends = []
        for d in range(1, nc):
            k = lax.rem(chip + d, nc)
            sends.append(remote(block, block, ag_s.at[g, d], ag_r.at[g, d], 2 * k + core))
            sends[-1].start()
        ag.append(sends)
        fw.append([remote(block, block, fw_s.at[g, 0], fw_r.at[g, 0], partner)])
        fw[g][0].start()

    back = jnp.zeros(hx.shape, F32)
    for g in range(pieces):
        cols = pl.ds(g * cut, cut)
        for d in range(1, nc):
            ag[g][d - 1].wait_recv()
            k = lax.rem(chip + nc - d, nc)
            block = ga.at[core * nc + k, :, cols]
            fw[g].append(remote(block, block, fw_s.at[g, d], fw_r.at[g, d], partner))
            fw[g][d].start()
        for copy in fw[g]:
            copy.wait_recv()
        back = back + lax.dot_general(
            flat_rows(ga[:, :, cols]), head_v[:, g * cut:(g + 1) * cut],
            (((1,), (1,)), ((), ())), preferred_element_type=F32,
        )
    gap_copy = pltpu.make_async_copy(ga, gap_out, out_sem.at[3])
    gap_copy.start()
    bk[...] = back.reshape(bk.shape)

    dest = lax.div(i, group)
    source = lax.rem(i, group) * nv + v
    fins = []
    for d in range(n):
        j = lax.rem(i + d, n)
        fins.append(
            remote(bk.at[slot(j)], fin.at[source], fin_s.at[d], fin_r.at[source], j, dest)
        )
    stays = dest == v
    self_copy = pltpu.make_async_copy(bk.at[mine], fin.at[source], fin_r.at[source])
    for d in range(1, n):
        fins[d].start()

    @pl.when(stays)
    def _():
        self_copy.start()

    @pl.when(jnp.logical_not(stays))
    def _():
        fins[0].start()

    for q in range(n):
        pltpu.make_async_copy(fin.at[q], fin.at[q], fin_r.at[q]).wait()
    wide = hx.shape[1]
    for r in range(group):
        grad = fin[r * nv]
        for q in range(1, nv):
            grad = grad + fin[r * nv + q]
        grad_out[:, r * wide:(r + 1) * wide] = grad.astype(BF16)

    for copy in hid + emb + idc + pair + sts + fins[1:]:
        copy.wait_send()
    for sends in rs + ag + fw:
        for copy in sends:
            copy.wait_send()

    @pl.when(jnp.logical_not(stays))
    def _():
        fins[0].wait_send()

    hid_copy.wait()
    emb_copy.wait()
    ids_copy.wait()
    gap_copy.wait()


def head_grad_kernel(hid, emb, ids, gap, out, lhs):
    step = pl.program_id(0)
    tokens = hid.shape[0] * hid.shape[1]
    width = out.shape[1]

    @pl.when(step == 0)
    def _():
        both = jnp.concatenate(
            [a[...].astype(F32).reshape(tokens, a.shape[2]) for a in (hid, emb)], axis=0
        )
        lhs[...] = both.T.astype(BF16)

    first = (lax.axis_index("vocab") * pl.num_programs(0) + step) * width
    column = lax.broadcasted_iota(jnp.int32, (tokens, width), 1) + first
    token = ids[...].reshape(tokens, ids.shape[2])[:, 0:1]
    lookup = jnp.where(column == token, 1.0, 0.0)
    rhs = jnp.concatenate([gap[...].astype(F32).reshape(tokens, width), lookup], axis=0)
    out[...] = jnp.dot(lhs[...], rhs.astype(BF16), preferred_element_type=F32)


def per_device(n, nv, hidden, embed_grad, token_ids, loss_weight, teacher_logits, head):
    rows, model = hidden.shape
    wide, vocab = head.shape
    nc = n // 2
    chunks = 8 if n <= 8 else 4
    pieces = 4
    tokens = n * rows

    def blocks(a):
        return a.reshape(rows, n, wide).swapaxes(0, 1)

    dma = pltpu.SemaphoreType.DMA
    any_spec = pl.BlockSpec(memory_space=pl.ANY)
    vmem_spec = pl.BlockSpec(memory_space=pltpu.VMEM)
    smem_spec = pl.BlockSpec(memory_space=pltpu.SMEM)
    grad_hidden, gap, hid, emb, ids = pl.pallas_call(
        functools.partial(comm_kernel, n, nv, chunks, pieces),
        out_shape=(
            jax.ShapeDtypeStruct((rows, model // nv), BF16),
            jax.ShapeDtypeStruct((n, rows, vocab), BF16),
            jax.ShapeDtypeStruct((n, rows, wide), BF16),
            jax.ShapeDtypeStruct((n, rows, wide), BF16),
            jax.ShapeDtypeStruct((n, rows, 128), jnp.int32),
        ),
        in_specs=[any_spec, any_spec, smem_spec, smem_spec, any_spec, any_spec],
        out_specs=(vmem_spec, any_spec, any_spec, any_spec, any_spec),
        scratch_shapes=[
            pltpu.VMEM((n, rows, wide), BF16),
            pltpu.VMEM((n, rows, wide), BF16),
            pltpu.VMEM((n, rows, 128), jnp.int32),
            pltpu.VMEM((rows, vocab), BF16),
            pltpu.VMEM((wide, vocab), BF16),
            pltpu.VMEM((tokens, wide), BF16),
            pltpu.VMEM((chunks, 2, nc, rows, vocab // chunks), F32),
            pltpu.VMEM((chunks, nc, rows, vocab // chunks), F32),
            pltpu.VMEM((chunks, nc, rows, vocab // chunks), F32),
            pltpu.VMEM((chunks, nc, rows, vocab // chunks), F32),
            pltpu.VMEM((rows, vocab), F32),
            pltpu.VMEM((nv, rows, 128), F32),
            pltpu.VMEM((n, rows, vocab), BF16),
            pltpu.VMEM((n, rows, wide), F32),
            pltpu.VMEM((n, rows, wide), F32),
            dma((chunks,)), dma, dma((2,)), dma((4,)),
            dma((n,)), dma((n,)), dma((n,)), dma((n,)), dma((n,)), dma((n,)),
            dma((chunks,)), dma((chunks,)),
            dma((chunks, nc)), dma((chunks, nc)),
            dma((nv,)), dma((nv,)),
            dma((pieces, nc)), dma((pieces, nc)), dma((pieces, nc)), dma((pieces, nc)),
            dma((n,)), dma((n,)),
        ],
        compiler_params=pltpu.CompilerParams(
            collective_id=0, has_side_effects=True, vmem_limit_bytes=64_000_000
        ),
        name="exchange",
    )(blocks(hidden), blocks(embed_grad), token_ids, loss_weight, teacher_logits, head)

    steps = 8
    cols = vocab // steps
    head_grad = pl.pallas_call(
        head_grad_kernel,
        grid=(steps,),
        out_shape=jax.ShapeDtypeStruct((wide, vocab), F32),
        in_specs=[
            pl.BlockSpec((n, rows, wide), lambda s: (0, 0, 0)),
            pl.BlockSpec((n, rows, wide), lambda s: (0, 0, 0)),
            pl.BlockSpec((n, rows, 128), lambda s: (0, 0, 0)),
            pl.BlockSpec((n, rows, cols), lambda s: (0, 0, s)),
        ],
        out_specs=pl.BlockSpec((wide, cols), lambda s: (0, s)),
        scratch_shapes=[pltpu.VMEM((wide, 2 * tokens), BF16)],
        compiler_params=pltpu.CompilerParams(vmem_limit_bytes=40_000_000),
        name="head_grad",
    )(hid, emb, ids, gap)
    return grad_hidden, head_grad


def solution(mesh):
    placed = (P("dp", None), P("dp", None), P("dp"), P("dp"), P("dp", "vocab"), P("dp", "vocab"))
    return jax.shard_map(
        functools.partial(per_device, mesh.shape["dp"], mesh.shape["vocab"]),
        mesh=mesh,
        in_specs=placed,
        out_specs=(P("dp", "vocab"), P("dp", "vocab")),
        check_vma=False,
    )
```

time: 175 us -> 67.1 us (0.38)
  Pallas kernels: 0 us -> 61.9 us
  waiting for transfers between devices: 59.4 us -> 0 us
  matrix products: 35.9 us -> 0 us
  blocking collectives: 30.3 us -> 0 us
  local copies, waits for them, and re-layouts: 20 us -> 4.26 us
  between operations: 15.2 us -> 0.65 us
  starting transfers between devices: 6.86 us -> 0 us
  other arithmetic: 6.1 us -> 0 us
    pallas_call x0 -> x2, Pallas kernels: none -> 61.9 us  [the longest x1 53.8 us: per_device(): pl.pallas_call(functools.partial(comm_kernel, n, nv, chunks, pieces), out...]
    reduce_scatter x2 -> x0, waiting for transfers between devices: 38.6 us -> none  [the longest x1 38.6 us: per_device(): lax.psum_scatter(jnp.dot(hidden_cols, head, preferred_element_type=jnp.fl...]
    dot_general x4 -> x0, matrix products: 35.9 us -> none  [the longest x2 22.5 us: contract_rows(): lax.dot_general(left, right, (((0,), (0,)), ((), ())), preferred_element_...]
    all_gather x1 -> x0, waiting for transfers between devices: 20.8 us -> none  [per_device(): gap_piece = lax.all_gather(gap, 'dp', axis=0, tiled=True)]
    unnamed x2 -> x0, blocking collectives: 20.1 us -> none
    unnamed x26 -> x11, local copies, waits for them, and re-layouts: 19.6 us -> 4.26 us
    all_to_all x1 -> x0, blocking collectives: 10.2 us -> none  [per_device(): lax.all_to_all(hidden, 'dp', split_axis=1, concat_axis=0, tiled=True)]
    all_to_all x2 -> x0, starting transfers between devices: 6.74 us -> none  [the longest x1 3.37 us: per_device(): lax.all_to_all(back_cols, 'dp', split_axis=0, concat_axis=1, tiled=True)]
  transfers between devices with their start and end apart: 5 -> 0, of which waited for: 2 -> 0; matrix products, arithmetic and copies ran while one was open for 24% -> 0% of each run, Pallas kernels for 0% -> 0%
where the time goes in v1:
time: 67.1 us; the launch traced here: 66.8 us
  Pallas kernels  61.9 us (92%)
  local copies, waits for them, and re-layouts  4.26 us (6%)
    pallas_call x1, Pallas kernels, per_device(): pl.pallas_call(functools.partial(comm_kernel, n, nv, chunks, pieces), out...  53.8 us
    pallas_call x1, Pallas kernels, per_device(): pl.pallas_call(head_grad_kernel, grid=(steps,), out_shape=jax.ShapeDtypeS...  8.06 us
    unnamed x11, local copies, waits for them, and re-layouts  4.26 us

profile of v1, /device:TPU:0, one launch (start us, length us, event | category | flops | bytes accessed | tf_op | source)
XLA Modules:
  0.0 66.8 jit_solution(5356524534678215915)
XLA Ops:
  0.6 53.8 %exchange.1 = (bf16[8,1024]{1,0:T(8,128)(2,1)}, bf16[8,8,8192]{2,1,0:T(8,128)(2,1)}, bf16[8,8,512]{2,1,0:T(8,128)(2,1)}, bf16[8,8,512]{2,1,0:T(8,128)(2,1)}, s32[8,8,128]{2,1,0:T(8,128)}) custom-call(bf16[8,8,512]{2,1,0:T(8,128)(2,1)} %bitcast.6, bf16[8,8,512]{2,1,0:T(8,128)(2,1)} %bitcast.7, s32[8]{0:T(128)} %ids.1, f32[8]{0:T(128)} %weight.1, ...), custom_call_target="tpu_custom_call" | custom-call | tf_op jit(solution)/shard_map/exchange/pallas_call | solution.py:292
  54.4 0.0 copy-start
  54.5 1.2 %copy-done = bf16[8,8,8192]{2,1,0:T(8,128)(2,1)S(1)} copy-done((bf16[8,8,8192]{2,1,0:T(8,128)(2,1)S(1)}, bf16[8,8,8192]{2,1,0:T(8,128)(2,1)}, u32[]{:S(2)}) %copy-start) | copy-done | bytes 1048600
  55.7 0.0 copy-start.1
  55.7 0.8 %copy-done.1 = bf16[8,8,512]{2,1,0:T(8,128)(2,1)S(1)} copy-done((bf16[8,8,512]{2,1,0:T(8,128)(2,1)S(1)}, bf16[8,8,512]{2,1,0:T(8,128)(2,1)}, u32[]{:S(2)}) %copy-start.1) | copy-done | bytes 65560
  56.5 0.0 copy-start.2
  56.5 0.8 %copy-done.2 = bf16[8,8,512]{2,1,0:T(8,128)(2,1)S(1)} copy-done((bf16[8,8,512]{2,1,0:T(8,128)(2,1)S(1)}, bf16[8,8,512]{2,1,0:T(8,128)(2,1)}, u32[]{:S(2)}) %copy-start.2) | copy-done | bytes 65560
  57.3 0.0 copy-start.3
  57.4 0.8 %copy-done.3 = s32[8,8,128]{2,1,0:T(8,128)S(1)} copy-done((s32[8,8,128]{2,1,0:T(8,128)S(1)}, s32[8,8,128]{2,1,0:T(8,128)}, u32[]{:S(2)}) %copy-start.3) | copy-done | bytes 32792
  58.1 0.0 copy-start.4
  58.1 8.1 %head_grad.1 = f32[512,8192]{1,0:T(8,128)} custom-call(bf16[8,8,512]{2,1,0:T(8,128)(2,1)S(1)} %copy-done.1, bf16[8,8,512]{2,1,0:T(8,128)(2,1)S(1)} %copy-done.2, s32[8,8,128]{2,1,0:T(8,128)S(1)} %copy-done.3, bf16[8,8,8192]{2,1,0:T(8,128)(2,1)S(1)} %copy-done), custom_call_target="tpu_custom_call" | custom-call | tf_op jit(solution)/shard_map/head_grad/pallas_call | solution.py:335
  66.2 0.0 copy-done.4
  66.2 0.6 copy.9
Async XLA Ops:
  54.4 1.2 %copy-start = (bf16[8,8,8192]{2,1,0:T(8,128)(2,1)S(1)}, bf16[8,8,8192]{2,1,0:T(8,128)(2,1)}, u32[]{:S(2)}) copy-start(bf16[8,8,8192]{2,1,0:T(8,128)(2,1)} %get-tuple-element.11.gap) | copy-start | bytes 3145732
  55.7 0.8 %copy-start.1 = (bf16[8,8,512]{2,1,0:T(8,128)(2,1)S(1)}, bf16[8,8,512]{2,1,0:T(8,128)(2,1)}, u32[]{:S(2)}) copy-start(bf16[8,8,512]{2,1,0:T(8,128)(2,1)} %get-tuple-element.8.hid) | copy-start | bytes 196612
  56.5 0.8 %copy-start.2 = (bf16[8,8,512]{2,1,0:T(8,128)(2,1)S(1)}, bf16[8,8,512]{2,1,0:T(8,128)(2,1)}, u32[]{:S(2)}) copy-start(bf16[8,8,512]{2,1,0:T(8,128)(2,1)} %get-tuple-element.9.emb) | copy-start | bytes 196612
  57.3 0.8 %copy-start.3 = (s32[8,8,128]{2,1,0:T(8,128)S(1)}, s32[8,8,128]{2,1,0:T(8,128)}, u32[]{:S(2)}) copy-start(s32[8,8,128]{2,1,0:T(8,128)} %get-tuple-element.10.ids) | copy-start | bytes 98308
  58.1 8.1 %copy-start.4 = (bf16[8,1024]{1,0:T(8,128)(2,1)S(1)}, bf16[8,1024]{1,0:T(8,128)(2,1)}, u32[]{:S(2)}) copy-start(bf16[8,1024]{1,0:T(8,128)(2,1)} %get-tuple-element.14) | copy-start | bytes 49156

commit v2 on v1

--- a/solution.py
+++ b/solution.py
@@ -20,10 +20,10 @@
     n, nv, chunks, pieces,
     hidden, embed, ids, weight, teacher, head,
     grad_out, gap_out, hid_out, emb_out, ids_out,
-    hc, ec, idt, tea, head_v, hx, part, xbuf, total, rsbuf, stu, stat, ga, bk, fin,
+    hc, ec, idt, tea, head_v, hx, part, xbuf, total, rsbuf, stu, stat, ga, bk, bq, fin,
     head_sem, tea_sem, own_sem, out_sem,
     hid_s, hid_r, emb_s, emb_r, ids_s, ids_r,
-    pair_s, pair_r, rs_s, rs_r, st_s, st_r, ag_s, ag_r, fw_s, fw_r, fin_s, fin_r,
+    pair_s, pair_r, rs_s, rs_r, st_s, st_r, ag_s, ag_r, fw_s, fw_r, row_s, row_r, fin_s, fin_r,
 ):
     i = lax.axis_index("dp")
     v = lax.axis_index("vocab")
@@ -48,14 +48,10 @@
         )
 
     barrier = pltpu.get_barrier_semaphore()
-    for dd in range(n):
-        for dv in range(nv):
-            if dd or dv:
-                pl.semaphore_signal(
-                    barrier, inc=1,
-                    device_id=(lax.rem(i + dd, n), lax.rem(v + dv, nv)),
-                    device_id_type=MESH,
-                )
+    peers = [(lax.rem(i + d, n), v) for d in range(1, n)]
+    peers += [(i, lax.rem(v + d, nv)) for d in range(1, nv)]
+    for peer in peers:
+        pl.semaphore_signal(barrier, inc=1, device_id=peer, device_id_type=MESH)
 
     own = [
         pltpu.make_async_copy(hidden.at[i], hc.at[mine], own_sem.at[0]),
@@ -80,7 +76,7 @@
     idt[mine] = id_tile
     w_col = w_tile[:, 0:1]
 
-    pl.semaphore_wait(barrier, n * nv - 1)
+    pl.semaphore_wait(barrier, len(peers))
 
     hid, emb, idc = [], [], []
     for d in range(1, n):
@@ -208,45 +204,38 @@
     gap_copy.start()
     bk[...] = back.reshape(bk.shape)
 
-    dest = lax.div(i, group)
-    source = lax.rem(i, group) * nv + v
+    self_copy = pltpu.make_async_copy(bk.at[mine], bq.at[i], row_r.at[i])
+    self_copy.start()
+    rows_out = []
+    for d in range(1, n):
+        j = lax.rem(i + d, n)
+        rows_out.append(remote(bk.at[slot(j)], bq.at[i], row_s.at[d], row_r.at[i], j))
+        rows_out[-1].start()
     fins = []
-    for d in range(n):
-        j = lax.rem(i + d, n)
-        fins.append(
-            remote(bk.at[slot(j)], fin.at[source], fin_s.at[d], fin_r.at[source], j, dest)
-        )
-    stays = dest == v
-    self_copy = pltpu.make_async_copy(bk.at[mine], fin.at[source], fin_r.at[source])
-    for d in range(1, n):
-        fins[d].start()
-
-    @pl.when(stays)
-    def _():
-        self_copy.start()
-
-    @pl.when(jnp.logical_not(stays))
-    def _():
-        fins[0].start()
-
-    for q in range(n):
-        pltpu.make_async_copy(fin.at[q], fin.at[q], fin_r.at[q]).wait()
+    for d in range(1, nv + 1):
+        u = lax.rem(v + d, nv)
+        for r in range(group):
+            q = u * group + r
+            pltpu.make_async_copy(bq.at[q], bq.at[q], row_r.at[q]).wait()
+        if d < nv:
+            fins.append(
+                remote(bq.at[pl.ds(u * group, group)], fin.at[d], fin_s.at[d], fin_r.at[d], i, u)
+            )
+            fins[-1].start()
+    for copy in fins:
+        copy.wait_recv()
     wide = hx.shape[1]
     for r in range(group):
-        grad = fin[r * nv]
-        for q in range(1, nv):
-            grad = grad + fin[r * nv + q]
+        grad = bq[v * group + r]
+        for d in range(1, nv):
+            grad = grad + fin[d, r]
         grad_out[:, r * wide:(r + 1) * wide] = grad.astype(BF16)
 
-    for copy in hid + emb + idc + pair + sts + fins[1:]:
+    for copy in hid + emb + idc + pair + sts + rows_out + fins:
         copy.wait_send()
     for sends in rs + ag + fw:
         for copy in sends:
             copy.wait_send()
-
-    @pl.when(jnp.logical_not(stays))
-    def _():
-        fins[0].wait_send()
 
     hid_copy.wait()
     emb_copy.wait()
@@ -316,13 +305,14 @@
             pltpu.VMEM((n, rows, vocab), BF16),
             pltpu.VMEM((n, rows, wide), F32),
             pltpu.VMEM((n, rows, wide), F32),
+            pltpu.VMEM((nv, n // nv, rows, wide), F32),
             dma((chunks,)), dma, dma((2,)), dma((4,)),
             dma((n,)), dma((n,)), dma((n,)), dma((n,)), dma((n,)), dma((n,)),
             dma((chunks,)), dma((chunks,)),
             dma((chunks, nc)), dma((chunks, nc)),
             dma((nv,)), dma((nv,)),
             dma((pieces, nc)), dma((pieces, nc)), dma((pieces, nc)), dma((pieces, nc)),
-            dma((n,)), dma((n,)),
+            dma((n,)), dma((n,)), dma((nv,)), dma((nv,)),
         ],
         compiler_params=pltpu.CompilerParams(
             collective_id=0, has_side_effects=True, vmem_limit_bytes=64_000_000
@@ -344,7 +334,7 @@
         ],
         out_specs=pl.BlockSpec((wide, cols), lambda s: (0, s)),
         scratch_shapes=[pltpu.VMEM((wide, 2 * tokens), BF16)],
-        compiler_params=pltpu.CompilerParams(vmem_limit_bytes=40_000_000),
+        compiler_params=pltpu.CompilerParams(vmem_limit_bytes=64_000_000),
         name="head_grad",
     )(hid, emb, ids, gap)
     return grad_hidden, head_grad

time: 67.1 us -> 60.3 us (0.90)
  local copies, waits for them, and re-layouts: 4.26 us -> 0.61 us
  Pallas kernels: 61.9 us -> 58.8 us
    pallas_call x1, Pallas kernels: 53.8 us -> 49.5 us  [per_device(): pl.pallas_call(functools.partial(comm_kernel, n, nv, chunks, pieces), out...]
    unnamed x11 -> x3, local copies, waits for them, and re-layouts: 4.26 us -> 0.61 us
    pallas_call x1, Pallas kernels: 8.06 us -> 9.34 us  [per_device(): pl.pallas_call(head_grad_kernel, grid=(steps,), out_shape=jax.ShapeDtypeS...]
where the time goes in v2:
time: 60.3 us; the launch traced here: 60.1 us
  Pallas kernels  58.8 us (98%)
  between operations  0.65 us (1%)
  local copies, waits for them, and re-layouts  0.61 us (1%)
    pallas_call x1, Pallas kernels, per_device(): pl.pallas_call(functools.partial(comm_kernel, n, nv, chunks, pieces), out...  49.5 us
    pallas_call x1, Pallas kernels, per_device(): pl.pallas_call(head_grad_kernel, grid=(steps,), out_shape=jax.ShapeDtypeS...  9.34 us

profile of v2, /device:TPU:0, one launch (start us, length us, event | category | flops | bytes accessed | tf_op | source)
XLA Modules:
  0.0 60.1 jit_solution(3324221862354734142)
XLA Ops:
  0.6 49.5 %exchange.1 = (bf16[8,1024]{1,0:T(8,128)(2,1)}, bf16[8,8,8192]{2,1,0:T(8,128)(2,1)}, bf16[8,8,512]{2,1,0:T(8,128)(2,1)}, bf16[8,8,512]{2,1,0:T(8,128)(2,1)}, s32[8,8,128]{2,1,0:T(8,128)}) custom-call(bf16[8,8,512]{2,1,0:T(8,128)(2,1)} %bitcast.6, bf16[8,8,512]{2,1,0:T(8,128)(2,1)} %bitcast.7, s32[8]{0:T(128)} %ids.1, f32[8]{0:T(128)} %weight.1, ...), custom_call_target="tpu_custom_call" | custom-call | tf_op jit(solution)/shard_map/exchange/pallas_call | solution.py:281
  50.1 0.0 copy-start
  50.1 9.3 %head_grad.1 = f32[512,8192]{1,0:T(8,128)} custom-call(bf16[8,8,512]{2,1,0:T(8,128)(2,1)} %get-tuple-element.8.hid, bf16[8,8,512]{2,1,0:T(8,128)(2,1)} %get-tuple-element.9.emb, s32[8,8,128]{2,1,0:T(8,128)} %get-tuple-element.10.ids, bf16[8,8,8192]{2,1,0:T(8,128)(2,1)} %get-tuple-element.11.gap), custom_call_target="tpu_custom_call" | custom-call | tf_op jit(solution)/shard_map/head_grad/pallas_call | solution.py:325
  59.4 0.0 copy-done
  59.5 0.6 %copy.9 = bf16[8,1024]{1,0:T(8,128)(2,1)} copy(bf16[8,1024]{1,0:T(8,128)(2,1)S(1)} %copy-done) | data formatting | bytes 32768
Async XLA Ops:
  50.1 9.4 %copy-start = (bf16[8,1024]{1,0:T(8,128)(2,1)S(1)}, bf16[8,1024]{1,0:T(8,128)(2,1)}, u32[]{:S(2)}) copy-start(bf16[8,1024]{1,0:T(8,128)(2,1)} %get-tuple-element.14) | copy-start | bytes 49156
